TPU v7x, 32 devices: a whole 2x2x4 slice. The times are simulated.
32 devices in a mesh: replica: 4 (over y, core), fsdp: 8 (over z, x).
Axes of the slice: x: 2, y: 2, z: 4, core: 2. Of those that a mesh axis runs over, the one named last changes fastest.
Arguments:
- hidden_states: bfloat16 [4, 2048, 4096], P('replica', 'fsdp'), may hold values from -6 to 6
- norm_gain: bfloat16 [4, 4096], P('replica', 'fsdp'), may hold values from 0.5 to 1.5
- key_weight: bfloat16 [4, 4096, 1024], P('replica', 'fsdp'), may hold values from -0.09375 to 0.09375
- value_weight: bfloat16 [4, 4096, 1024], P('replica', 'fsdp'), may hold values from -0.09375 to 0.09375
- deltas: float32 [4, 256, 4096], P('replica', 'fsdp'), may hold values from -6 to 6
- outer_params: float32 [256, 4096], P('fsdp', 'replica'), may hold values from -6 to 6
- momentum: float32 [256, 4096], P('fsdp', 'replica'), may hold values from -3 to 3
- local_params: bfloat16 [4, 256, 4096], P('replica', 'fsdp'), may hold values from -6 to 6
Outputs:
- keys: bfloat16 [4, 2048, 1024], P('replica', 'fsdp')
- values: bfloat16 [4, 2048, 1024], P('replica', 'fsdp')
- momentum_new: float32 [256, 4096], P('fsdp', 'replica')
- outer_new: float32 [256, 4096], P('fsdp', 'replica')
- local_new: bfloat16 [4, 256, 4096], P('replica', 'fsdp')
All inputs are finite; a program needn't handle non-finite values.
Results may differ from a plain program's by a relative error of at most 0.0085.
Values may be sent and summed in bfloat16 or wider, within the bound.
A program may use at most 128 MiB of HBM per device.

v0:
```python
import jax
import jax.numpy as jnp
from jax import lax
from jax.sharding import PartitionSpec as P

HEAD = 128


def rotate_keys(keys_raw, positions, head_size):
    half_width = head_size // 2
    exponent = jnp.arange(half_width, dtype=jnp.float32) * (2.0 / head_size)
    frequency = jnp.power(jnp.float32(500000.0), -exponent)
    angles = positions.astype(jnp.float32)[:, None] * frequency[None, :]
    cosine_table = jnp.cos(angles)[:, None, :]
    sine_table = jnp.sin(angles)[:, None, :]
    shaped = keys_raw.reshape(keys_raw.shape[0], -1, head_size)
    first_half = shaped[:, :, :half_width]
    second_half = shaped[:, :, half_width:]
    turned = jnp.concatenate(
        [
            first_half * cosine_table - second_half * sine_table,
            second_half * cosine_table + first_half * sine_table,
        ],
        axis=2,
    )
    return turned.reshape(keys_raw.shape)


def per_device(
    hidden_states, norm_gain, key_weight, value_weight, deltas, outer_params, momentum, local_params
):
    states = hidden_states[0]
    squares = jnp.square(states.astype(jnp.float32))
    inv_rms = lax.rsqrt(jnp.mean(squares, axis=1, keepdims=True) + 1e-05)
    gain_rows = lax.all_gather(norm_gain[0], "fsdp", axis=0, tiled=True)
    key_rows = lax.all_gather(key_weight[0], "fsdp", axis=0, tiled=True)
    value_rows = lax.all_gather(value_weight[0], "fsdp", axis=0, tiled=True)
    normed = (states.astype(jnp.float32) * inv_rms * gain_rows.astype(jnp.float32)[None, :]).astype(
        jnp.bfloat16
    )
    keys_raw = jnp.dot(normed, key_rows, preferred_element_type=jnp.float32)
    values_raw = jnp.dot(normed, value_rows, preferred_element_type=jnp.float32)
    positions = jnp.arange(states.shape[0], dtype=jnp.int32)
    rotated = rotate_keys(keys_raw, positions, HEAD)
    replicas = lax.axis_size("replica")
    delta_rows = deltas[0]
    avg_whole = lax.psum(delta_rows.astype(jnp.bfloat16), "replica").astype(jnp.float32) / replicas
    outer_whole = lax.all_gather(outer_params, "replica", axis=1, tiled=True)
    momentum_whole = lax.all_gather(momentum, "replica", axis=1, tiled=True)
    momentum_full = 0.9 * momentum_whole + avg_whole
    outer_rows = outer_whole - 0.7 * (avg_whole + 0.9 * momentum_full)
    width_own = outer_params.shape[1]
    offset = lax.axis_index("replica") * width_own
    momentum_new = lax.dynamic_slice_in_dim(momentum_full, offset, width_own, 1)
    outer_new = lax.dynamic_slice_in_dim(outer_rows, offset, width_own, 1)
    local_new = (0.5 * local_params[0].astype(jnp.float32) + 0.5 * outer_rows).astype(jnp.bfloat16)[
        None
    ]
    return (
        rotated.astype(jnp.bfloat16)[None],
        values_raw.astype(jnp.bfloat16)[None],
        momentum_new,
        outer_new,
        local_new,
    )


def solution(mesh):
    in_specs = (
        P("replica", "fsdp", None),
        P("replica", "fsdp"),
        P("replica", "fsdp", None),
        P("replica", "fsdp", None),
        P("replica", "fsdp", None),
        P("fsdp", "replica"),
        P("fsdp", "replica"),
        P("replica", "fsdp", None),
    )
    out_specs = (
        P("replica", "fsdp", None),
        P("replica", "fsdp", None),
        P("fsdp", "replica"),
        P("fsdp", "replica"),
        P("replica", "fsdp", None),
    )
    return jax.shard_map(
        per_device, mesh=mesh, in_specs=in_specs, out_specs=out_specs, check_vma=False
    )
```

profile of v0, /device:TPU:0, one launch (start us, length us, event | category | flops | bytes accessed | tf_op | source)
XLA Modules:
  0.0 278.0 jit_solution(17915847253404958928)
XLA Ops:
  8.0 0.0 copy-start
  8.0 0.0 copy-start.1
  8.0 0.0 all-reduce.2.cloned.1.call-start
  8.1 1.9 convert_bitcast_fusion.1
  10.0 0.0 all-reduce.2.cloned.1.call-update
  10.0 0.0 all-gather.6.cloned.1.call-start
  10.1 0.5 all-gather.6.cloned.1.call-update
  10.6 0.0 all-gather.8.cloned.1.call-start
  10.6 0.5 all-gather.8.cloned.1.call-update
  11.2 28.9 %all-gather = bf16[1,4096]{1,0:T(2,128)(2,1)S(1)} all-gather(bf16[1,512]{1,0:T(2,128)(2,1)} %param.9), channel_id=2, replica_groups=mesh['replica'=4,'fsdp'=8] {'fsdp'}, dimensions={1}, use_global_device_ids=true | all-gather | bytes 9216 | tf_op jit(solution)/shard_map/all_gather | solution.py:35
  40.2 7.8 %all_gather.19 = f32[32,4096]{1,0:T(8,128)S(1)} all-gather(f32[32,1024]{1,0:T(8,128)} %param.13), channel_id=1, replica_groups=mesh['replica'=4,'fsdp'=8] {'replica'}, dimensions={1}, use_global_device_ids=true | all-gather | bytes 655360 | tf_op jit(solution)/shard_map/all_gather | solution.py:48
  47.9 7.5 %all_gather.18 = f32[32,4096]{1,0:T(8,128)S(1)} all-gather(f32[32,1024]{1,0:T(8,128)} %param.14), channel_id=1, replica_groups=mesh['replica'=4,'fsdp'=8] {'replica'}, dimensions={1}, use_global_device_ids=true | all-gather | bytes 655360 | tf_op jit(solution)/shard_map/all_gather | solution.py:49
  55.4 0.0 copy-done
  55.4 0.5 fusion.4
  55.9 0.6 add_rsqrt_fusion
  56.5 0.3 multiply_cosine_fusion
  56.8 0.0 all-reduce.2.cloned.1.call-done
  56.8 0.0 copy-done.1
  56.8 1.9 fusion.30
  58.7 0.7 constant_dynamic-slice_fusion
  59.4 80.3 %all-gather.6.cloned.1.call-done = bf16[1,4096,1024]{2,1,0:T(8,128)(2,1)} async-done(((bf16[1,512,1024]{2,1,0:T(8,128)(2,1)}), bf16[1,4096,1024]{2,1,0:T(8,128)(2,1)}) %all-gather.6.cloned.1.call-update) | async-done | bytes 8388624 | tf_op jit(solution)/shard_map/all_gather | solution.py:36
  139.7 0.0 copy-start.2
  139.7 11.4 %copy.13 = bf16[1024,4096]{1,0:T(8,128)(2,1)} copy(bf16[1024,4096]{0,1:T(8,128)(2,1)} %bitcast.44) | data formatting | bytes 16777216 | tf_op jit(solution)/shard_map/dot_general | solution.py:41
  151.1 0.0 copy-done.2
  151.1 5.8 %fusion.10 = f32[256,8,128]{0,2,1:T(8,128)S(1)} fusion(bf16[8,128,4096]{2,1,0:T(8,128)(2,1)} %bitcast.45, bf16[1,256,4096]{2,1,0:T(8,128)(2,1)S(1)} %copy-done, f32[4096]{0:T(1024)S(1)} %bitcast.47, f32[256]{0:T(256)S(1)} %copy-done.2), kind=kOutput, calls=%fused_computation.12 | convolution fusion | flops 2151677952 | bytes 11551744 | tf_op jit(solution)/shard_map/dot_general | solution.py:41
  156.9 0.1 subtract_convert_fusion
  157.1 1.0 copy.14
  158.1 105.9 %all-gather.8.cloned.1.call-done = bf16[1,4096,1024]{2,1,0:T(8,128)(2,1)} async-done(((bf16[1,512,1024]{2,1,0:T(8,128)(2,1)}), bf16[1,4096,1024]{2,1,0:T(8,128)(2,1)}) %all-gather.8.cloned.1.call-update) | async-done | bytes 8388624 | tf_op jit(solution)/shard_map/all_gather | solution.py:37
  264.0 6.6 %fusion.22 = bf16[1,256,1024]{2,1,0:T(8,128)(2,1)} fusion(bf16[1,4096,1024]{2,1,0:T(8,128)(2,1)} %all-gather.8.cloned.1.call-done, bf16[1,256,4096]{2,1,0:T(8,128)(2,1)S(1)} %copy-done, f32[4096]{0:T(1024)S(1)} %bitcast.48, f32[256]{0:T(256)S(1)} %copy-done.2), kind=kOutput, calls=%fused_computation.18 | convolution fusion | flops 2151940096 | bytes 11027456 | tf_op jit(solution)/shard_map/dot_general | solution.py:42
  (4 shorter events, 0.1 us)
Async XLA Ops:
  8.0 47.4 %copy-start = (bf16[1,256,4096]{2,1,0:T(8,128)(2,1)S(1)}, bf16[1,256,4096]{2,1,0:T(8,128)(2,1)}, u32[]{:S(2)}) copy-start(bf16[1,256,4096]{2,1,0:T(8,128)(2,1)} %param.8) | copy-start | bytes 6291460
  8.0 48.8 %copy-start.1 = (bf16[1,32,4096]{2,1,0:T(8,128)(2,1)S(1)}, bf16[1,32,4096]{2,1,0:T(8,128)(2,1)}, u32[]{:S(2)}) copy-start(bf16[1,32,4096]{2,1,0:T(8,128)(2,1)} %param.15) | copy-start | bytes 786436
  8.0 48.8 %all-reduce.2.cloned.1.call-start = ((), (), s32[]{:S(2)}) async-start(), calls=%async_computation | async-start | bytes 524288 | tf_op jit(solution)/shard_map/psum | solution.py:47
  10.0 129.7 %all-gather.6.cloned.1.call-start = ((), (), s32[]{:S(2)}) async-start(), calls=%async_computation.1 | async-start | bytes 9437184 | tf_op jit(solution)/shard_map/all_gather | solution.py:36
  10.6 253.4 %all-gather.8.cloned.1.call-start = ((), (), s32[]{:S(2)}) async-start(), calls=%async_computation.2 | async-start | bytes 9437184 | tf_op jit(solution)/shard_map/all_gather | solution.py:37
  139.7 11.4 %copy-start.2 = (f32[256]{0:T(256)S(1)}, f32[256]{0:T(256)}, u32[]{:S(2)}) copy-start(f32[256]{0:T(256)} %add_rsqrt_fusion) | copy-start | bytes 3076
Sparse Core Ops, SparseCore 0:
  11.7 35.1 all-reduce.1
Sparse Core Ops, SparseCore 1:
  12.6 127.0 all-gather.5
  141.7 122.3 all-gather.7
where the time goes:
time: 279 us; the launch traced here: 278 us
  waiting for transfers between devices  187 us (67%)
  blocking collectives  44.2 us (16%)
  between operations  15.6 us (6%)
  local copies, waits for them, and re-layouts  13.2 us (5%)
  matrix products  12.4 us (4%)
  other arithmetic  5.36 us (2%)
    all_gather x1, waiting for transfers between devices, per_device(): value_rows = lax.all_gather(value_weight[0], 'fsdp', axis=0, tiled=True)  106 us
    all_gather x1, waiting for transfers between devices, per_device(): key_rows = lax.all_gather(key_weight[0], 'fsdp', axis=0, tiled=True)  80.3 us
    all_gather x1, blocking collectives, per_device(): gain_rows = lax.all_gather(norm_gain[0], 'fsdp', axis=0, tiled=True)  28.9 us
    dot_general x1, local copies, waits for them, and re-layouts, per_device(): keys_raw = jnp.dot(normed, key_rows, preferred_element_type=jnp.float32)  11.4 us
    all_gather x1, blocking collectives, per_device(): outer_whole = lax.all_gather(outer_params, 'replica', axis=1, tiled=True)  7.78 us
    all_gather x1, blocking collectives, per_device(): momentum_whole = lax.all_gather(momentum, 'replica', axis=1, tiled=True)  7.48 us
    dot_general x1, matrix products, per_device(): values_raw = jnp.dot(normed, value_rows, preferred_element_type=jnp.float32)  6.55 us
    dot_general x1, matrix products, per_device(): keys_raw = jnp.dot(normed, key_rows, preferred_element_type=jnp.float32)  5.82 us
  transfers between devices with their start and end apart: 3, of which 2 were waited for; matrix products, arithmetic and copies ran while one was open for 8% of the time, Pallas kernels for 0%

commit v1 on v0

--- a/solution.py
+++ b/solution.py
@@ -45,8 +45,13 @@
     replicas = lax.axis_size("replica")
     delta_rows = deltas[0]
     avg_whole = lax.psum(delta_rows.astype(jnp.bfloat16), "replica").astype(jnp.float32) / replicas
-    outer_whole = lax.all_gather(outer_params, "replica", axis=1, tiled=True)
-    momentum_whole = lax.all_gather(momentum, "replica", axis=1, tiled=True)
+    outer_whole, momentum_whole = jnp.split(
+        lax.all_gather(
+            jnp.concatenate([outer_params, momentum], axis=0), "replica", axis=1, tiled=True
+        ),
+        [outer_params.shape[0]],
+        axis=0,
+    )
     momentum_full = 0.9 * momentum_whole + avg_whole
     outer_rows = outer_whole - 0.7 * (avg_whole + 0.9 * momentum_full)
     width_own = outer_params.shape[1]

time: 279 us -> 330 us (1.18)
  waiting for transfers between devices: 187 us -> 255 us
  blocking collectives: 44.2 us -> 28.1 us
    all_gather x1, waiting for transfers between devices: 80.3 us -> 124 us  [per_device(): key_rows = lax.all_gather(key_weight[0], 'fsdp', axis=0, tiled=True)]
    all_gather x0 -> x1, waiting for transfers between devices: none -> 18.9 us  [per_device(): lax.all_gather(jnp.concatenate([outer_params, momentum], axis=0), 'replic...]
    all_gather x2 -> x0, blocking collectives: 15.3 us -> none  [the longest x1 7.78 us: per_device(): outer_whole = lax.all_gather(outer_params, 'replica', axis=1, tiled=True)]
    psum x1, waiting for transfers between devices: 0.02 us -> 4.72 us  [per_device(): lax.psum(delta_rows.astype(jnp.bfloat16), 'replica').astype(jnp.float32)]
  transfers between devices with their start and end apart: 3 -> 4, of which waited for: 2 -> 4; matrix products, arithmetic and copies ran while one was open for 8% -> 7% of each run, Pallas kernels for 0% -> 0%
where the time goes in v1:
time: 330 us; the launch traced here: 329 us
  waiting for transfers between devices  255 us (77%)
  blocking collectives  28.1 us (9%)
  between operations  13.8 us (4%)
  local copies, waits for them, and re-layouts  13.2 us (4%)
  matrix products  12.4 us (4%)
  other arithmetic  6.8 us (2%)
    all_gather x1, waiting for transfers between devices, per_device(): key_rows = lax.all_gather(key_weight[0], 'fsdp', axis=0, tiled=True)  124 us
    all_gather x1, waiting for transfers between devices, per_device(): value_rows = lax.all_gather(value_weight[0], 'fsdp', axis=0, tiled=True)  106 us
    all_gather x1, blocking collectives, per_device(): gain_rows = lax.all_gather(norm_gain[0], 'fsdp', axis=0, tiled=True)  28.1 us
    all_gather x1, waiting for transfers between devices, per_device(): lax.all_gather(jnp.concatenate([outer_params, momentum], axis=0), 'replic...  18.9 us
    dot_general x1, local copies, waits for them, and re-layouts, per_device(): keys_raw = jnp.dot(normed, key_rows, preferred_element_type=jnp.float32)  11.4 us
  transfers between devices with their start and end apart: 4, of which 4 were waited for; matrix products, arithmetic and copies ran while one was open for 7% of the time, Pallas kernels for 0%

profile of v1, /device:TPU:0, one launch (start us, length us, event | category | flops | bytes accessed | tf_op | source)
XLA Modules:
  0.0 329.2 jit_solution(14298136896830572760)
XLA Ops:
  7.2 0.0 copy-start
  7.2 0.0 copy-start.1
  7.2 0.0 all-reduce.2.cloned.1.call-start
  7.2 1.9 convert_bitcast_fusion.1
  9.2 0.0 all-reduce.2.cloned.1.call-update
  9.2 0.0 all-gather.7.cloned.1.call-start
  9.2 1.7 pad_maximum_fusion.1
  10.9 0.0 all-gather.7.cloned.1.call-update
  10.9 0.0 all-gather.9.cloned.1.call-start
  11.0 0.7 all-gather.9.cloned.1.call-update
  11.7 0.0 all-gather.11.cloned.1.call-start
  11.7 0.5 all-gather.11.cloned.1.call-update
  12.3 28.1 %all-gather = bf16[1,4096]{1,0:T(2,128)(2,1)S(1)} all-gather(bf16[1,512]{1,0:T(2,128)(2,1)} %param.9), channel_id=2, replica_groups=mesh['replica'=4,'fsdp'=8] {'fsdp'}, dimensions={1}, use_global_device_ids=true | all-gather | bytes 9216 | tf_op jit(solution)/shard_map/all_gather | solution.py:35
  40.4 0.0 copy-done
  40.4 0.5 fusion.4
  40.9 0.3 multiply_cosine_fusion
  41.2 4.7 %all-reduce.2.cloned.1.call-done = bf16[32,4096]{1,0:T(8,128)(2,1)} async-done(((bf16[32,4096]{1,0:T(8,128)(2,1)}), bf16[32,4096]{1,0:T(8,128)(2,1)}) %all-reduce.2.cloned.1.call-update) | async-done | bytes 262160 | tf_op jit(solution)/shard_map/psum | solution.py:47
  45.9 18.9 %all-gather.7.cloned.1.call-done = f32[64,4096]{1,0:T(8,128)} async-done(((f32[64,1024]{1,0:T(8,128)}), f32[64,4096]{1,0:T(8,128)}) %all-gather.7.cloned.1.call-update) | async-done | bytes 1048592 | tf_op jit(solution)/shard_map/all_gather | solution.py:49
  64.8 0.0 copy-done.1
  64.8 2.2 fusion.30
  67.0 0.7 constant_dynamic-slice_fusion
  67.7 123.7 %all-gather.9.cloned.1.call-done = bf16[1,4096,1024]{2,1,0:T(8,128)(2,1)} async-done(((bf16[1,512,1024]{2,1,0:T(8,128)(2,1)}), bf16[1,4096,1024]{2,1,0:T(8,128)(2,1)}) %all-gather.9.cloned.1.call-update) | async-done | bytes 8388624 | tf_op jit(solution)/shard_map/all_gather | solution.py:36
  191.4 11.4 %copy.13 = bf16[1024,4096]{1,0:T(8,128)(2,1)} copy(bf16[1024,4096]{0,1:T(8,128)(2,1)} %bitcast.44) | data formatting | bytes 16777216 | tf_op jit(solution)/shard_map/dot_general | solution.py:41
  202.9 5.8 %fusion.10 = f32[256,8,128]{0,2,1:T(8,128)S(1)} fusion(bf16[8,128,4096]{2,1,0:T(8,128)(2,1)} %bitcast.45, bf16[1,256,4096]{2,1,0:T(8,128)(2,1)S(1)} %copy-done, f32[4096]{0:T(1024)S(1)} %bitcast.47, f32[256]{0:T(256)S(1)} %add_rsqrt_fusion), kind=kOutput, calls=%fused_computation.12 | convolution fusion | flops 2151677952 | bytes 11551744 | tf_op jit(solution)/shard_map/dot_general | solution.py:41
  208.7 0.1 subtract_convert_fusion
  208.9 1.0 copy.14
  209.9 106.2 %all-gather.11.cloned.1.call-done = bf16[1,4096,1024]{2,1,0:T(8,128)(2,1)} async-done(((bf16[1,512,1024]{2,1,0:T(8,128)(2,1)}), bf16[1,4096,1024]{2,1,0:T(8,128)(2,1)}) %all-gather.11.cloned.1.call-update) | async-done | bytes 8388624 | tf_op jit(solution)/shard_map/all_gather | solution.py:37
  316.1 6.6 %fusion.22 = bf16[1,256,1024]{2,1,0:T(8,128)(2,1)} fusion(bf16[1,4096,1024]{2,1,0:T(8,128)(2,1)} %all-gather.11.cloned.1.call-done, bf16[1,256,4096]{2,1,0:T(8,128)(2,1)S(1)} %copy-done, f32[4096]{0:T(1024)S(1)} %bitcast.48, f32[256]{0:T(256)S(1)} %add_rsqrt_fusion), kind=kOutput, calls=%fused_computation.18 | convolution fusion | flops 2151940096 | bytes 11027456 | tf_op jit(solution)/shard_map/dot_general | solution.py:42
  (5 shorter events, 0.1 us)
Async XLA Ops:
  7.2 33.2 %copy-start = (bf16[1,256,4096]{2,1,0:T(8,128)(2,1)S(1)}, bf16[1,256,4096]{2,1,0:T(8,128)(2,1)}, u32[]{:S(2)}) copy-start(bf16[1,256,4096]{2,1,0:T(8,128)(2,1)} %param.8) | copy-start | bytes 6291460
  7.2 57.6 %copy-start.1 = (bf16[1,32,4096]{2,1,0:T(8,128)(2,1)S(1)}, bf16[1,32,4096]{2,1,0:T(8,128)(2,1)}, u32[]{:S(2)}) copy-start(bf16[1,32,4096]{2,1,0:T(8,128)(2,1)} %param.15) | copy-start | bytes 786436
  7.2 38.7 %all-reduce.2.cloned.1.call-start = ((), (), s32[]{:S(2)}) async-start(), calls=%async_computation.1 | async-start | bytes 524288 | tf_op jit(solution)/shard_map/psum | solution.py:47
  9.2 55.6 %all-gather.7.cloned.1.call-start = ((), (), s32[]{:S(2)}) async-start(), calls=%async_computation | async-start | bytes 1310720 | tf_op jit(solution)/shard_map/all_gather | solution.py:49
  10.9 180.5 %all-gather.9.cloned.1.call-start = ((), (), s32[]{:S(2)}) async-start(), calls=%async_computation.2 | async-start | bytes 9437184 | tf_op jit(solution)/shard_map/all_gather | solution.py:36
  11.7 304.4 %all-gather.11.cloned.1.call-start = ((), (), s32[]{:S(2)}) async-start(), calls=%async_computation.3 | async-start | bytes 9437184 | tf_op jit(solution)/shard_map/all_gather | solution.py:37
Sparse Core Ops, SparseCore 0:
  10.9 34.9 all-reduce.1
  48.1 16.6 all-gather.6
  66.9 124.4 all-gather.8
  193.4 122.6 all-gather.10
